TPU v7x, 32 devices: a whole 2x2x4 slice. The times are simulated.
32 devices in a mesh: expert: 4 (over z), shard: 8 (over y, x, core).
Axes of the slice: x: 2, y: 2, z: 4, core: 2. Of those that a mesh axis runs over, the one named last changes fastest.
Arguments:
- master_down: float32 [16, 6400, 4096], P('expert', None, 'shard'), may hold values from -0.109375 to 0.109375
- second_down: bfloat16 [16, 6400, 4096], P('expert', None, 'shard'), may hold values from -0.0390625 to 0.0390625
- router_weight: float32 [4096, 16], P('shard', 'expert'), may hold values from -0.09375 to 0.09375
- router_gain: float32 [4096], P('shard'), may hold values from 0.25 to 1.75
Outputs:
- final_down: bfloat16 [16, 6400, 4096], P('expert', 'shard')
- scale_down: float32 [16, 6400], P('expert', 'shard')
- serve_router: bfloat16 [4096, 16], replicated
All inputs are finite; a program needn't handle non-finite values.
Results may differ from a plain program's by a relative error of at most 0.001.
Values may be sent and summed in bfloat16 or wider, within the bound.
A program may use at most 256 MiB of HBM per device.

v0:
```python
import jax
import jax.numpy as jnp
from jax import lax
from jax.sharding import PartitionSpec as P


def local(master_down, second_down, router_weight, router_gain):
    merged_down = master_down + second_down.astype(jnp.float32)
    total_down = lax.psum(jnp.sum(merged_down * merged_down, axis=2), "shard")
    scale_down = jnp.sqrt(total_down)
    narrow_down = (merged_down / jnp.expand_dims(scale_down, 2)).astype(jnp.bfloat16)
    final_down = lax.all_to_all(narrow_down, "shard", split_axis=1, concat_axis=2, tiled=True)
    scale_down = lax.dynamic_slice_in_dim(
        scale_down, lax.axis_index("shard") * final_down.shape[1], final_down.shape[1], axis=1
    )
    part_router = (router_weight * router_gain[:, None]).astype(jnp.bfloat16)
    row_router = lax.all_gather(part_router, "shard", axis=0, tiled=True)
    serve_router = lax.all_gather(row_router, "expert", axis=1, tiled=True)
    return (final_down, scale_down, serve_router)


def solution(mesh):
    return jax.shard_map(
        local,
        mesh=mesh,
        in_specs=(
            P("expert", None, "shard"),
            P("expert", None, "shard"),
            P("shard", "expert"),
            P("shard"),
        ),
        out_specs=(P("expert", "shard", None), P("expert", "shard"), P()),
        check_vma=False,
    )
```

profile of v0, /device:TPU:0, one launch (start us, length us, event | category | flops | bytes accessed | tf_op | source)
XLA Modules:
  0.0 554.8 jit_solution(7517493062815123618)
XLA Ops:
  7.2 0.0 all-reduce.2.cloned.1.call-start
  7.2 24.2 %multiply_reduce_fusion = f32[4,6400]{1,0:T(4,128)S(1)} fusion(f32[4,6400,512]{2,1,0:T(8,128)} %param.4, bf16[4,6400,512]{2,1,0:T(8,128)(2,1)} %param.5), kind=kLoop, calls=%fused_computation.1 | loop fusion | flops 52403200 | bytes 78745600 | tf_op jit(solution)/shard_map/reduce_sum | solution.py:9
  31.4 2.3 copy.21
  33.7 0.0 all-reduce.2.cloned.1.call-update
  33.7 73.6 %all-reduce.2.cloned.1.call-done = f32[4,6400]{0,1:T(8,128)} async-done(((f32[4,6400]{0,1:T(8,128)}), f32[4,6400]{0,1:T(8,128)}) %all-reduce.2.cloned.1.call-update) | async-done | bytes 102416 | tf_op jit(solution)/shard_map/psum | solution.py:9
  107.3 2.7 sqrt.3
  110.0 1.2 copy.17
  111.3 34.3 %divide_convert_fusion = bf16[4,6400,512]{2,1,0:T(8,128)(2,1)} fusion(f32[4,6400,512]{2,1,0:T(8,128)} %param.4, bf16[4,6400,512]{2,1,0:T(8,128)(2,1)} %param.5, f32[4,6400]{1,0:T(4,128)S(1)} %copy.17), kind=kLoop, calls=%fused_computation | loop fusion | flops 52428800 | bytes 104960000 | tf_op jit(solution)/shard_map/convert_element_type | solution.py:11
  145.5 33.4 %copy.18 = bf16[4,6400,512]{2,0,1:T(4,128)(2,1)} copy(bf16[4,6400,512]{2,1,0:T(8,128)(2,1)} %divide_convert_fusion) | data formatting | bytes 52428800 | tf_op jit(solution)/shard_map/convert_element_type | solution.py:11
  178.9 0.0 copy-start
  178.9 0.0 copy-start.1
  178.9 6.6 %all-to-all-start = ((bf16[4,6400,512]{2,0,1:T(4,128)(2,1)}), bf16[4,6400,512]{2,0,1:T(4,128)(2,1)}, u32[]{:S(2)}, u32[]{:S(2)}) async-start(bf16[4,6400,512]{2,0,1:T(4,128)(2,1)} %copy.18), calls=%async_computation | async-start | bytes 52428800 | tf_op jit(solution)/shard_map/all_to_all | solution.py:12
  185.6 0.0 copy-done
  185.6 0.0 copy-done.1
  185.6 288.2 %all_gather.6 = bf16[4096,4]{0,1:T(4,128)(2,1)S(1)} all-gather(bf16[512,4]{0,1:T(4,128)(2,1)S(1)} %multiply_convert_fusion), channel_id=1, replica_groups=mesh['expert'=4,'shard'=8] {'shard'}, dimensions={0}, use_global_device_ids=true | all-gather | bytes 36864 | tf_op jit(solution)/shard_map/all_gather | solution.py:17
  473.8 13.5 %all-gather = bf16[4,4,4096]{2,1,0:T(4,128)(2,1)S(1)} all-gather(bf16[1,4,4096]{2,1,0:T(4,128)(2,1)S(1)} %bitcast.9), channel_id=1, replica_groups=mesh['expert'=4,'shard'=8] {'expert'}, dimensions={0}, use_global_device_ids=true | all-gather | bytes 163840 | tf_op jit(solution)/shard_map/all_gather | solution.py:18
  487.3 0.7 reshape.9
  488.0 0.8 constant_dynamic-slice_fusion
  488.7 1.8 copy.20
  490.5 0.0 all-to-all-done
  490.5 18.2 %copy.19 = bf16[4,800,8,512]{3,2,1,0:T(8,128)(2,1)} copy(bf16[4,800,8,512]{3,0,1,2:T(4,128)(2,1)} %bitcast.1) | data formatting | bytes 52428800 | tf_op jit(solution)/shard_map/all_to_all | solution.py:12
  508.7 39.2 %all_to_all.16 = bf16[4,800,4096]{2,1,0:T(8,128)(2,1)} reshape(bf16[4,800,8,512]{3,2,1,0:T(8,128)(2,1)} %copy.19) | data formatting | bytes 52428800 | tf_op jit(solution)/shard_map/all_to_all | solution.py:12
  (1 shorter events, 0.0 us)
Async XLA Ops:
  7.2 100.2 %all-reduce.2.cloned.1.call-start = ((), (), s32[]{:S(2)}) async-start(), calls=%async_computation.1 | async-start | bytes 6553600 | tf_op jit(solution)/shard_map/psum | solution.py:9
  178.9 6.7 %copy-start = (f32[512,4]{0,1:T(4,128)S(1)}, f32[512,4]{0,1:T(4,128)}, u32[]{:S(2)}) copy-start(f32[512,4]{0,1:T(4,128)} %param.6) | copy-start | bytes 24580
  178.9 6.7 %copy-start.1 = (f32[512]{0:T(512)S(1)}, f32[512]{0:T(512)}, u32[]{:S(2)}) copy-start(f32[512]{0:T(512)} %param.7) | copy-start | bytes 6148
  178.9 311.6 %all-to-all-start = ((bf16[4,6400,512]{2,0,1:T(4,128)(2,1)}), bf16[4,6400,512]{2,0,1:T(4,128)(2,1)}, u32[]{:S(2)}, u32[]{:S(2)}) async-start(bf16[4,6400,512]{2,0,1:T(4,128)(2,1)} %copy.18), calls=%async_computation | async-start | bytes 52428800 | tf_op jit(solution)/shard_map/all_to_all | solution.py:12
Sparse Core Ops, SparseCore 0:
  33.9 73.4 all-reduce.1
where the time goes:
time: 556 us; the launch traced here: 555 us
  blocking collectives  302 us (54%)
  local copies, waits for them, and re-layouts  100 us (18%)
  waiting for transfers between devices  73.6 us (13%)
  other arithmetic  58.5 us (11%)
  between operations  14.1 us (3%)
  starting transfers between devices  6.67 us (1%)
    all_gather x1, blocking collectives, local(): row_router = lax.all_gather(part_router, 'shard', axis=0, tiled=True)  288 us
    psum x1, waiting for transfers between devices, local(): total_down = lax.psum(jnp.sum(merged_down * merged_down, axis=2), 'shard')  73.6 us
    all_to_all x2, local copies, waits for them, and re-layouts, local(): lax.all_to_all(narrow_down, 'shard', split_axis=1, concat_axis=2, tiled=T...  57.4 us
    convert_element_type x1, other arithmetic, local(): (merged_down / jnp.expand_dims(scale_down, 2)).astype(jnp.bfloat16)  34.3 us
    convert_element_type x1, local copies, waits for them, and re-layouts, local(): (merged_down / jnp.expand_dims(scale_down, 2)).astype(jnp.bfloat16)  33.4 us
    reduce_sum x1, other arithmetic, local(): total_down = lax.psum(jnp.sum(merged_down * merged_down, axis=2), 'shard')  24.2 us
    all_gather x1, blocking collectives, local(): serve_router = lax.all_gather(row_router, 'expert', axis=1, tiled=True)  13.5 us
  transfers between devices with their start and end apart: 2, of which 1 were waited for; matrix products, arithmetic and copies ran while one was open for 1% of the time, Pallas kernels for 0%

commit v1 on v0

--- a/solution.py
+++ b/solution.py
@@ -6,7 +6,9 @@
 
 def local(master_down, second_down, router_weight, router_gain):
     merged_down = master_down + second_down.astype(jnp.float32)
-    total_down = lax.psum(jnp.sum(merged_down * merged_down, axis=2), "shard")
+    total_down = jnp.sum(
+        lax.all_gather(jnp.sum(merged_down * merged_down, axis=2), "shard"), axis=0
+    )
     scale_down = jnp.sqrt(total_down)
     narrow_down = (merged_down / jnp.expand_dims(scale_down, 2)).astype(jnp.bfloat16)
     final_down = lax.all_to_all(narrow_down, "shard", split_axis=1, concat_axis=2, tiled=True)

time: 556 us -> 475 us (0.85)
  waiting for transfers between devices: 73.6 us -> 0.01 us
  between operations: 14.1 us -> 0.71 us
  blocking collectives: 302 us -> 314 us
    psum x1 -> x0, waiting for transfers between devices: 73.6 us -> none  [local(): total_down = lax.psum(jnp.sum(merged_down * merged_down, axis=2), 'shard')]
    all_gather x0 -> x1, blocking collectives: none -> 12 us  [local(): lax.all_gather(jnp.sum(merged_down * merged_down, axis=2), 'shard')]
    reduce_sum x1 -> x2, other arithmetic: 24.2 us -> 24.4 us  [the longest x1 24.2 us: local(): jnp.sum(merged_down * merged_down, axis=2)]
  transfers between devices with their start and end apart: 2 -> 1, of which waited for: 1 -> 0; matrix products, arithmetic and copies ran while one was open for 1% -> 0% of each run, Pallas kernels for 0% -> 0%
where the time goes in v1:
time: 475 us; the launch traced here: 474 us
  blocking collectives  314 us (66%)
  local copies, waits for them, and re-layouts  94.5 us (20%)
  other arithmetic  58.7 us (12%)
  starting transfers between devices  6.5 us (1%)
    all_gather x1, blocking collectives, local(): row_router = lax.all_gather(part_router, 'shard', axis=0, tiled=True)  288 us
    all_to_all x2, local copies, waits for them, and re-layouts, local(): lax.all_to_all(narrow_down, 'shard', split_axis=1, concat_axis=2, tiled=T...  57.4 us
    convert_element_type x1, other arithmetic, local(): (merged_down / jnp.expand_dims(scale_down, 2)).astype(jnp.bfloat16)  34.3 us
    convert_element_type x1, local copies, waits for them, and re-layouts, local(): (merged_down / jnp.expand_dims(scale_down, 2)).astype(jnp.bfloat16)  33.4 us
    reduce_sum x1, other arithmetic, local(): jnp.sum(merged_down * merged_down, axis=2)  24.2 us
    all_gather x1, blocking collectives, local(): serve_router = lax.all_gather(row_router, 'expert', axis=1, tiled=True)  13.6 us
    all_gather x1, blocking collectives, local(): lax.all_gather(jnp.sum(merged_down * merged_down, axis=2), 'shard')  12 us
  transfers between devices with their start and end apart: 1, of which 0 were waited for; matrix products, arithmetic and copies ran while one was open for 0% of the time, Pallas kernels for 0%

profile of v1, /device:TPU:0, one launch (start us, length us, event | category | flops | bytes accessed | tf_op | source)
XLA Modules:
  0.0 474.2 jit_solution(13347673864453672481)
XLA Ops:
  0.6 24.2 %multiply_reduce_fusion = f32[4,6400]{1,0:T(4,128)S(1)} fusion(f32[4,6400,512]{2,1,0:T(8,128)} %param.4, bf16[4,6400,512]{2,1,0:T(8,128)(2,1)} %param.5), kind=kLoop, calls=%fused_computation.1 | loop fusion | flops 52403200 | bytes 78745600 | tf_op jit(solution)/shard_map/reduce_sum | solution.py:10
  24.9 1.1 copy.21
  26.0 1.2 copy.18
  27.2 12.0 %all-gather.1 = f32[8,4,6400]{2,1,0:T(4,128)S(1)} all-gather(f32[1,4,6400]{2,1,0:T(4,128)S(1)} %copy.18), channel_id=2, replica_groups=mesh['expert'=4,'shard'=8] {'shard'}, dimensions={0}, use_global_device_ids=true | all-gather | bytes 921600 | tf_op jit(solution)/shard_map/all_gather | solution.py:10
  39.2 0.1 reduce_sum.19
  39.4 0.1 sqrt.7
  39.4 34.3 %divide_convert_fusion = bf16[4,6400,512]{2,1,0:T(8,128)(2,1)} fusion(f32[4,6400,512]{2,1,0:T(8,128)} %param.4, bf16[4,6400,512]{2,1,0:T(8,128)(2,1)} %param.5, f32[4,6400]{1,0:T(4,128)S(1)} %sqrt.7), kind=kLoop, calls=%fused_computation | loop fusion | flops 52428800 | bytes 104960000 | tf_op jit(solution)/shard_map/convert_element_type | solution.py:13
  73.7 0.0 copy-start
  73.7 0.0 copy-start.1
  73.7 33.4 %copy.19 = bf16[4,6400,512]{2,0,1:T(4,128)(2,1)} copy(bf16[4,6400,512]{2,1,0:T(8,128)(2,1)} %divide_convert_fusion) | data formatting | bytes 52428800 | tf_op jit(solution)/shard_map/convert_element_type | solution.py:13
  107.1 6.5 %all-to-all-start = ((bf16[4,6400,512]{2,0,1:T(4,128)(2,1)}), bf16[4,6400,512]{2,0,1:T(4,128)(2,1)}, u32[]{:S(2)}, u32[]{:S(2)}) async-start(bf16[4,6400,512]{2,0,1:T(4,128)(2,1)} %copy.19), calls=%async_computation | async-start | bytes 52428800 | tf_op jit(solution)/shard_map/all_to_all | solution.py:14
  113.6 0.0 copy-done
  113.6 0.0 copy-done.1
  113.7 288.2 %all_gather.14 = bf16[4096,4]{0,1:T(4,128)(2,1)S(1)} all-gather(bf16[512,4]{0,1:T(4,128)(2,1)S(1)} %multiply_convert_fusion), channel_id=1, replica_groups=mesh['expert'=4,'shard'=8] {'shard'}, dimensions={0}, use_global_device_ids=true | all-gather | bytes 36864 | tf_op jit(solution)/shard_map/all_gather | solution.py:19
  401.8 13.6 %all-gather.2 = bf16[4,4,4096]{2,1,0:T(4,128)(2,1)S(1)} all-gather(bf16[1,4,4096]{2,1,0:T(4,128)(2,1)S(1)} %bitcast.11), channel_id=1, replica_groups=mesh['expert'=4,'shard'=8] {'expert'}, dimensions={0}, use_global_device_ids=true | all-gather | bytes 163840 | tf_op jit(solution)/shard_map/all_gather | solution.py:20
  415.4 0.7 reshape.14
  416.1 0.7 constant_dynamic-slice_fusion
  416.8 0.0 all-to-all-done
  416.8 18.2 %copy.20 = bf16[4,800,8,512]{3,2,1,0:T(8,128)(2,1)} copy(bf16[4,800,8,512]{3,0,1,2:T(4,128)(2,1)} %bitcast.2) | data formatting | bytes 52428800 | tf_op jit(solution)/shard_map/all_to_all | solution.py:14
  435.0 39.2 %all_to_all.16 = bf16[4,800,4096]{2,1,0:T(8,128)(2,1)} reshape(bf16[4,800,8,512]{3,2,1,0:T(8,128)(2,1)} %copy.20) | data formatting | bytes 52428800 | tf_op jit(solution)/shard_map/all_to_all | solution.py:14
  (1 shorter events, 0.0 us)
Async XLA Ops:
  73.7 39.9 %copy-start = (f32[512,4]{0,1:T(4,128)S(1)}, f32[512,4]{0,1:T(4,128)}, u32[]{:S(2)}) copy-start(f32[512,4]{0,1:T(4,128)} %param.6) | copy-start | bytes 24580
  73.7 39.9 %copy-start.1 = (f32[512]{0:T(512)S(1)}, f32[512]{0:T(512)}, u32[]{:S(2)}) copy-start(f32[512]{0:T(512)} %param.7) | copy-start | bytes 6148
  107.1 309.7 %all-to-all-start = ((bf16[4,6400,512]{2,0,1:T(4,128)(2,1)}), bf16[4,6400,512]{2,0,1:T(4,128)(2,1)}, u32[]{:S(2)}, u32[]{:S(2)}) async-start(bf16[4,6400,512]{2,0,1:T(4,128)(2,1)} %copy.19), calls=%async_computation | async-start | bytes 52428800 | tf_op jit(solution)/shard_map/all_to_all | solution.py:14

commit v2 on v0

--- a/solution.py
+++ b/solution.py
@@ -9,7 +9,12 @@
     total_down = lax.psum(jnp.sum(merged_down * merged_down, axis=2), "shard")
     scale_down = jnp.sqrt(total_down)
     narrow_down = (merged_down / jnp.expand_dims(scale_down, 2)).astype(jnp.bfloat16)
-    final_down = lax.all_to_all(narrow_down, "shard", split_axis=1, concat_axis=2, tiled=True)
+    final_down = jnp.concatenate(
+        lax.all_to_all(
+            jnp.stack(jnp.split(narrow_down, lax.axis_size("shard"), axis=1)), "shard", 0, 0
+        ),
+        axis=2,
+    )
     scale_down = lax.dynamic_slice_in_dim(
         scale_down, lax.axis_index("shard") * final_down.shape[1], final_down.shape[1], axis=1
     )

time: 556 us -> 488 us (0.88)
  local copies, waits for them, and re-layouts: 100 us -> 50.8 us
  waiting for transfers between devices: 73.6 us -> 54.9 us
    all_to_all x2 -> x0, local copies, waits for them, and re-layouts: 57.4 us -> none  [local(): lax.all_to_all(narrow_down, 'shard', split_axis=1, concat_axis=2, tiled=T...]
    convert_element_type x1 -> x0, local copies, waits for them, and re-layouts: 33.4 us -> none  [local(): (merged_down / jnp.expand_dims(scale_down, 2)).astype(jnp.bfloat16)]
    unnamed x7 -> x12, local copies, waits for them, and re-layouts: 4.75 us -> 27.5 us
    psum x1, waiting for transfers between devices: 73.6 us -> 54.9 us  [local(): total_down = lax.psum(jnp.sum(merged_down * merged_down, axis=2), 'shard')]
    reshape x0 -> x1, local copies, waits for them, and re-layouts: none -> 17.9 us  [local(): jnp.concatenate(lax.all_to_all(jnp.stack(jnp.split(narrow_down, lax.axis_...]
  transfers between devices with their start and end apart: 2 -> 2, of which waited for: 1 -> 1; matrix products, arithmetic and copies ran while one was open for 1% -> 0% of each run, Pallas kernels for 0% -> 0%
where the time goes in v2:
time: 488 us; the launch traced here: 487 us
  blocking collectives  302 us (62%)
  other arithmetic  59.2 us (12%)
  waiting for transfers between devices  54.9 us (11%)
  local copies, waits for them, and re-layouts  50.8 us (10%)
  between operations  14.1 us (3%)
  starting transfers between devices  6.66 us (1%)
    all_gather x1, blocking collectives, local(): row_router = lax.all_gather(part_router, 'shard', axis=0, tiled=True)  288 us
    psum x1, waiting for transfers between devices, local(): total_down = lax.psum(jnp.sum(merged_down * merged_down, axis=2), 'shard')  54.9 us
    convert_element_type x1, other arithmetic, local(): (merged_down / jnp.expand_dims(scale_down, 2)).astype(jnp.bfloat16)  34.3 us
    unnamed x12, local copies, waits for them, and re-layouts  27.5 us
    reduce_sum x1, other arithmetic, local(): total_down = lax.psum(jnp.sum(merged_down * merged_down, axis=2), 'shard')  24.9 us
    reshape x1, local copies, waits for them, and re-layouts, local(): jnp.concatenate(lax.all_to_all(jnp.stack(jnp.split(narrow_down, lax.axis_...  17.9 us
    all_gather x1, blocking collectives, local(): serve_router = lax.all_gather(row_router, 'expert', axis=1, tiled=True)  13.5 us
  transfers between devices with their start and end apart: 2, of which 1 were waited for; matrix products, arithmetic and copies ran while one was open for 0% of the time, Pallas kernels for 0%

profile of v2, /device:TPU:0, one launch (start us, length us, event | category | flops | bytes accessed | tf_op | source)
XLA Modules:
  0.0 487.3 jit_solution(10689226386606609922)
XLA Ops:
  7.2 0.0 all-reduce.2.cloned.1.call-start
  7.2 24.9 %multiply_reduce_fusion = f32[4,6400]{1,0:T(4,128)} fusion(f32[4,6400,512]{2,1,0:T(8,128)} %param.4, bf16[4,6400,512]{2,1,0:T(8,128)(2,1)} %param.5), kind=kLoop, calls=%fused_computation.1 | loop fusion | flops 52403200 | bytes 78745600 | tf_op jit(solution)/shard_map/reduce_sum | solution.py:9
  32.1 0.0 all-reduce.2.cloned.1.call-update
  32.1 54.9 %all-reduce.2.cloned.1.call-done = f32[4,6400]{1,0:T(4,128)} async-done(((f32[4,6400]{1,0:T(4,128)}), f32[4,6400]{1,0:T(4,128)}) %all-reduce.2.cloned.1.call-update) | async-done | bytes 102416 | tf_op jit(solution)/shard_map/psum | solution.py:9
  87.0 0.9 sqrt.3
  88.0 34.3 %divide_convert_fusion = bf16[4,6400,512]{2,1,0:T(8,128)(2,1)} fusion(f32[4,6400,512]{2,1,0:T(8,128)} %param.4, bf16[4,6400,512]{2,1,0:T(8,128)(2,1)} %param.5, f32[4,6400]{1,0:T(4,128)S(1)} %sqrt.3), kind=kLoop, calls=%fused_computation | loop fusion | flops 52428800 | bytes 104960000 | tf_op jit(solution)/shard_map/convert_element_type | solution.py:11
  122.2 3.8 fusion.7
  126.1 3.8 fusion.6
  129.9 3.8 fusion.5
  133.7 3.8 fusion.4
  137.6 3.9 fusion.3
  141.4 3.8 fusion.2
  145.2 3.8 fusion.1
  149.1 3.8 fusion
  152.9 0.0 copy-start
  152.9 0.0 copy-start.1
  152.9 6.6 %all-to-all-start = ((bf16[8,4,800,512]{3,2,1,0:T(8,128)(2,1)}), bf16[8,4,800,512]{3,2,1,0:T(8,128)(2,1)}, u32[]{:S(2)}, u32[]{:S(2)}) async-start(bf16[8,4,800,512]{3,2,1,0:T(8,128)(2,1)} %fusion), calls=%async_computation | async-start | bytes 52428800 | tf_op jit(solution)/shard_map/all_to_all | solution.py:13
  159.5 0.0 copy-done
  159.5 0.0 copy-done.1
  159.6 288.2 %all_gather.6 = bf16[4096,4]{0,1:T(4,128)(2,1)S(1)} all-gather(bf16[512,4]{0,1:T(4,128)(2,1)S(1)} %multiply_convert_fusion), channel_id=1, replica_groups=mesh['expert'=4,'shard'=8] {'shard'}, dimensions={0}, use_global_device_ids=true | all-gather | bytes 36864 | tf_op jit(solution)/shard_map/all_gather | solution.py:22
  447.7 13.5 %all-gather = bf16[4,4,4096]{2,1,0:T(4,128)(2,1)S(1)} all-gather(bf16[1,4,4096]{2,1,0:T(4,128)(2,1)S(1)} %bitcast.40), channel_id=1, replica_groups=mesh['expert'=4,'shard'=8] {'expert'}, dimensions={0}, use_global_device_ids=true | all-gather | bytes 163840 | tf_op jit(solution)/shard_map/all_gather | solution.py:23
  461.2 0.7 reshape.17
  461.9 0.7 constant_dynamic-slice_fusion
  462.6 0.0 all-to-all-done
  462.6 17.9 %copy.9 = bf16[8,4,100,8,512]{4,3,0,2,1:T(8,128)(2,1)} copy(bf16[8,4,100,8,512]{4,3,2,1,0:T(8,128)(2,1)} %bitcast.13) | data formatting | bytes 52428800 | tf_op jit(solution)/shard_map/reshape | solution.py:12
  (1 shorter events, 0.0 us)
Async XLA Ops:
  7.2 79.8 %all-reduce.2.cloned.1.call-start = ((), (), s32[]{:S(2)}) async-start(), calls=%async_computation.1 | async-start | bytes 204800 | tf_op jit(solution)/shard_map/psum | solution.py:9
  152.9 6.6 %copy-start = (f32[512,4]{0,1:T(4,128)S(1)}, f32[512,4]{0,1:T(4,128)}, u32[]{:S(2)}) copy-start(f32[512,4]{0,1:T(4,128)} %param.6) | copy-start | bytes 24580
  152.9 6.6 %copy-start.1 = (f32[512]{0:T(512)S(1)}, f32[512]{0:T(512)}, u32[]{:S(2)}) copy-start(f32[512]{0:T(512)} %param.7) | copy-start | bytes 6148
  152.9 309.7 %all-to-all-start = ((bf16[8,4,800,512]{3,2,1,0:T(8,128)(2,1)}), bf16[8,4,800,512]{3,2,1,0:T(8,128)(2,1)}, u32[]{:S(2)}, u32[]{:S(2)}) async-start(bf16[8,4,800,512]{3,2,1,0:T(8,128)(2,1)} %fusion), calls=%async_computation | async-start | bytes 52428800 | tf_op jit(solution)/shard_map/all_to_all | solution.py:13
Sparse Core Ops, SparseCore 0:
  32.2 54.7 all-reduce.1
